TPU v7x, 32 devices: a whole 2x2x4 slice. The times are simulated.
32 devices in a mesh: leaf: 4 (over x, core), blk: 8 (over z, y).
Axes of the slice: x: 2, y: 2, z: 4, core: 2. Of those that a mesh axis runs over, the one named last changes fastest.
Arguments:
- right_side: float32 [4, 4, 8, 384], P(None, 'leaf', 'blk'), may hold values from -6 to 6
- diag_inverse: bfloat16 [4, 8, 128, 7168], P('leaf', 'blk'), as said below
- update_factor: bfloat16 [4, 8, 128, 10240], P('leaf', 'blk'), may hold values from -0.09375 to 0.09375
- live_blocks: int32 [7], replicated, may hold values from 1 to 32, as said below
Outputs:
- forward_solution: float32 [4, 4, 8, 384], P(None, 'leaf', 'blk')
- solution: float32 [4, 4, 8, 384], P(None, 'leaf', 'blk')
Inputs may be any that keep to these rules, and one draw needn't show every extreme that they name: `live_blocks`: A supernode with 2^l * 8 block-rows (level l, listed level by level from level 0, by group within a level) has between a quarter of them (at least 1) and all of them live; the root supernode (the last entry) has all of them live. `diag_inverse`: each level's inverse diagonal block is lower triangular in its supernode's row order, with a positive diagonal.
All inputs are finite; a program needn't handle non-finite values.
Results may differ from a plain program's by a relative error of at most 0.009.
Values sent between devices are 32-bit elements; how exact they have to be, the bound alone decides.
No kernel may reach another device: no remote copies, remote signals or barrier semaphores. Data moves between devices by JAX's collectives and lax.ppermute only.
A program may use at most 128 MiB of HBM per device.

v0:
```python
import jax
import jax.numpy as jnp
from jax import lax
from jax.sharding import PartitionSpec as P


def swapped(block, axis, apart):
    count = lax.axis_size(axis)
    route = []
    for low in range(count):
        high = low | 1 << apart
        if high != low and high < count:
            route += [(low, high), (high, low)]
    return lax.ppermute(block, axis, route)


def group_sum(partial_value, height):
    current = lax.psum(partial_value, "blk")
    for bit_number in range(height):
        current = current + swapped(current, "leaf", bit_number)
    return current


def local(right_side, diag_inverse, update_factor, live_blocks):
    leaf_count = lax.axis_size("leaf")
    block_count = lax.axis_size("blk")
    levels = leaf_count.bit_length()
    leaf_index = lax.axis_index("leaf")
    block_index = lax.axis_index("blk")
    block_rows = diag_inverse.shape[2]
    vectors = right_side.shape[0]
    level_width = block_count * block_rows
    rows_all = leaf_count * level_width
    flat_side = right_side.reshape(vectors, 1, levels * block_rows)
    every_side = lax.all_gather(flat_side, ("leaf", "blk"), axis=1, tiled=True)
    inverse_rows = diag_inverse.reshape(block_rows, -1)
    update_rows = update_factor.reshape(block_rows, -1)
    orders = [(1 << height) * level_width for height in range(levels)]
    spans = [sum(orders[height + 1 :]) for height in range(levels)]
    update_start = [sum(spans[:height]) for height in range(levels)]
    contract_second = (((1,), (1,)), ((), ()))
    own_masks = []
    group_masks = []
    own_starts = []
    group_starts = []
    inverse_parts = []
    update_parts = []
    for height in range(levels):
        group_index = leaf_index >> height
        local_rank = leaf_index & (1 << height) - 1
        offset = 2 * leaf_count - (2 * leaf_count >> height)
        live_count = live_blocks[offset + group_index]
        own_position = local_rank * block_count + block_index
        own_masks.append((own_position < live_count).astype(jnp.float32))
        block_alive = (jnp.arange((1 << height) * block_count) < live_count).astype(jnp.float32)
        group_masks.append(jnp.repeat(block_alive, block_rows))
        own_starts.append(own_position * block_rows)
        group_starts.append(group_index * orders[height])
        start = ((1 << height) - 1) * level_width
        inverse_parts.append(inverse_rows[:, start : start + orders[height]])
        update_parts.append(
            update_rows[:, update_start[height] : update_start[height] + spans[height]]
        )
    pending = [jnp.zeros((vectors, orders[height]), jnp.float32) for height in range(levels)]
    forward = []
    for height in range(levels):
        level_side = every_side[:, :, height * block_rows : (height + 1) * block_rows].reshape(
            vectors, rows_all
        )
        source = lax.dynamic_slice_in_dim(level_side, group_starts[height], orders[height], 1)
        if height > 0:
            source = source - group_sum(pending[height], height)
        reduced = (group_masks[height] * source).astype(jnp.bfloat16)
        solved = own_masks[height] * lax.dot_general(
            reduced, inverse_parts[height], contract_second, preferred_element_type=jnp.float32
        )
        forward.append(solved)
        if height < levels - 1:
            spread = jnp.dot(
                solved.astype(jnp.bfloat16),
                update_parts[height],
                preferred_element_type=jnp.float32,
            )
            cursor = 0
            for ancestor in range(height + 1, levels):
                pending[ancestor] = (
                    pending[ancestor] + spread[:, cursor : cursor + orders[ancestor]]
                )
                cursor += orders[ancestor]
    whole_solved = [None] * levels
    backward = [None] * levels
    for height in reversed(range(levels)):
        residual = forward[height]
        if height < levels - 1:
            ancestors = jnp.concatenate(
                [whole_solved[ancestor] for ancestor in range(height + 1, levels)], axis=1
            )
            residual = residual - lax.dot_general(
                ancestors, update_parts[height], contract_second, preferred_element_type=jnp.float32
            )
        weighted = (own_masks[height] * residual).astype(jnp.bfloat16)
        partial_value = jnp.dot(weighted, inverse_parts[height], preferred_element_type=jnp.float32)
        supernode_solved = group_masks[height] * group_sum(partial_value, height)
        backward[height] = lax.dynamic_slice_in_dim(
            supernode_solved, own_starts[height], block_rows, 1
        )
        whole_solved[height] = supernode_solved.astype(jnp.bfloat16)
    forward_out = jnp.stack(forward, axis=1).reshape(vectors, 1, 1, levels * block_rows)
    backward_out = jnp.stack(backward, axis=1).reshape(vectors, 1, 1, levels * block_rows)
    return (forward_out, backward_out)


def solution(mesh):
    in_specs = (
        P(None, "leaf", "blk", None),
        P("leaf", "blk", None, None),
        P("leaf", "blk", None, None),
        P(),
    )
    out_specs = (P(None, "leaf", "blk", None), P(None, "leaf", "blk", None))
    return jax.shard_map(local, mesh=mesh, in_specs=in_specs, out_specs=out_specs, check_vma=False)
```

profile of v0, /device:TPU:0, one launch (start us, length us, event | category | flops | bytes accessed | tf_op | source)
XLA Modules:
  0.0 352.7 jit_solution(483365086368205140)
XLA Ops:
  7.2 0.0 copy-start
  7.2 0.0 all-reduce.3.cloned.1.call-start
  7.2 71.2 %all-gather = f32[4,32,1,384]{3,2,1,0:T(1,128)S(1)} all-gather(f32[4,1,1,384]{3,2,1,0:T(1,128)} %param.4), channel_id=2, replica_groups=mesh['leaf'=4,'blk'=8] {'leaf','blk'}, dimensions={1}, use_global_device_ids=true | all-gather | bytes 202752 | tf_op jit(solution)/shard_map/all_gather | solution.py:35
  78.5 1.4 fusion.53
  80.0 0.6 compare_convert_fusion.2
  80.6 0.1 broadcast_bitcast_fusion.2
  81.3 1.1 convolution_multiply_fusion.1
  82.5 1.7 fusion.2
  84.2 33.0 %psum.35 = f32[4,2048]{1,0:T(4,128)S(1)} all-reduce(f32[4,2048]{1,0:T(4,128)S(1)} %slice.44), channel_id=1, replica_groups=mesh['leaf'=4,'blk'=8] {'blk'}, use_global_device_ids=true, to_apply=%region_0.0 | all-reduce | flops 8192 | bytes 65536 | tf_op jit(solution)/shard_map/psum | solution.py:18
  117.2 0.0 collective-permute-start
  117.2 0.6 compare_convert_fusion.1
  117.9 0.1 broadcast_bitcast_fusion.1
  118.6 0.0 collective-permute-done
  118.6 0.0 copy-done
  118.6 0.2 convolution_multiply_fusion.2
  118.9 2.1 convolution_add_fusion
  121.0 0.0 all-reduce.3.cloned.1.call-update
  121.0 0.0 all-reduce.5.cloned.1.call-start
  121.1 65.9 %all-reduce.3.cloned.1.call-done = f32[4,4096]{1,0:T(4,128)} async-done(((f32[4,4096]{1,0:T(4,128)}), f32[4,4096]{1,0:T(4,128)}) %all-reduce.3.cloned.1.call-update) | async-done | bytes 65552 | tf_op jit(solution)/shard_map/psum | solution.py:18
  186.9 0.0 collective-permute-start.1
  186.9 0.6 compare_convert_fusion
  187.6 0.8 collective-permute-done.1
  188.4 0.9 add.75
  189.3 1.5 collective-permute-start.2
  190.8 0.1 broadcast_bitcast_fusion
  191.5 2.1 collective-permute-done.2
  193.6 0.4 convolution_multiply_fusion
  194.0 0.9 fusion.19
  194.9 0.0 all-reduce.5.cloned.1.call-update
  194.9 69.3 %all-reduce.5.cloned.1.call-done = f32[4,4096]{1,0:T(4,128)} async-done(((f32[4,4096]{1,0:T(4,128)}), f32[4,4096]{1,0:T(4,128)}) %all-reduce.5.cloned.1.call-update) | async-done | bytes 65552 | tf_op jit(solution)/shard_map/psum | solution.py:18
  264.2 0.0 collective-permute-start.3
  264.2 0.1 dynamic-slice
  264.3 1.4 collective-permute-done.3
  265.7 0.9 add.77
  266.5 1.5 collective-permute-start.4
  268.1 0.6 copy.6
  268.7 2.2 collective-permute-done.4
  270.9 1.9 fusion.18
  272.8 36.1 %psum.38 = f32[4,2048]{1,0:T(4,128)S(1)} all-reduce(f32[4,2048]{1,0:T(4,128)S(1)} %fusion.18), channel_id=1, replica_groups=mesh['leaf'=4,'blk'=8] {'blk'}, use_global_device_ids=true, to_apply=%region_3.0 | all-reduce | flops 8192 | bytes 65536 | tf_op jit(solution)/shard_map/psum | solution.py:18
  308.9 0.0 collective-permute-start.5
  308.9 1.2 collective-permute-done.5
  310.2 2.1 fusion.16
  312.3 33.0 %psum.39 = f32[4,1024]{1,0:T(4,128)S(1)} all-reduce(f32[4,1024]{1,0:T(4,128)S(1)} %fusion.16), channel_id=1, replica_groups=mesh['leaf'=4,'blk'=8] {'blk'}, use_global_device_ids=true, to_apply=%region_4.0 | all-reduce | flops 4096 | bytes 32768 | tf_op jit(solution)/shard_map/psum | solution.py:18
  345.3 0.6 copy.7
  (12 shorter events, 0.2 us)
Async XLA Ops:
  7.2 111.5 %copy-start = (bf16[1,1,128,7168]{3,2,1,0:T(8,128)(2,1)S(1)}, bf16[1,1,128,7168]{3,2,1,0:T(8,128)(2,1)}, u32[]{:S(2)}) copy-start(bf16[1,1,128,7168]{3,2,1,0:T(8,128)(2,1)} %param.5) | copy-start | bytes 5505028
  7.2 179.8 %all-reduce.3.cloned.1.call-start = ((), (), s32[]{:S(2)}) async-start(), calls=%async_computation | async-start | bytes 131072 | tf_op jit(solution)/shard_map/psum | solution.py:18
  117.2 1.4 collective-permute-start
  121.0 143.2 %all-reduce.5.cloned.1.call-start = ((), (), s32[]{:S(2)}) async-start(), calls=%async_computation.1 | async-start | bytes 131072 | tf_op jit(solution)/shard_map/psum | solution.py:18
  186.9 1.5 collective-permute-start.1
  189.3 4.3 %collective-permute-start.2 = (f32[4,4096]{1,0:T(4,128)S(1)}, f32[4,4096]{1,0:T(4,128)S(1)}, u32[]{:S(2)}, u32[]{:S(2)}) collective-permute-start(f32[4,4096]{1,0:T(4,128)S(1)} %add.75), channel_id=1, source_target_pairs={{0,16},{16,0},{8,24},{24,8},{1,17},{17,1},{9,25},{25,9},{2,18},{18... | collective-permute-start | bytes 196616 | tf_op jit(solution)/shard_map/ppermute | solution.py:14
  264.2 1.5 collective-permute-start.3
  266.5 4.3 %collective-permute-start.4 = (f32[4,4096]{1,0:T(4,128)S(1)}, f32[4,4096]{1,0:T(4,128)S(1)}, u32[]{:S(2)}, u32[]{:S(2)}) collective-permute-start(f32[4,4096]{1,0:T(4,128)S(1)} %add.77), channel_id=1, source_target_pairs={{0,16},{16,0},{8,24},{24,8},{1,17},{17,1},{9,25},{25,9},{2,18},{18... | collective-permute-start | bytes 196616 | tf_op jit(solution)/shard_map/ppermute | solution.py:14
  308.9 1.2 collective-permute-start.5
Sparse Core Ops, SparseCore 0:
  121.2 65.7 all-reduce.2
  195.0 69.1 all-reduce.4
where the time goes:
time: 353 us
  blocking collectives  173 us (49%)
  waiting for transfers between devices  143 us (41%)
  between operations  16.1 us (5%)
  matrix products  10.5 us (3%)
  other arithmetic  3.71 us (1%)
    psum x2, waiting for transfers between devices, group_sum(): current = lax.psum(partial_value, 'blk')  135 us
    psum x3, blocking collectives, group_sum(): current = lax.psum(partial_value, 'blk')  102 us
    all_gather x1, blocking collectives, local(): every_side = lax.all_gather(flat_side, ('leaf', 'blk'), axis=1, tiled=True)  71.2 us
    ppermute x6, waiting for transfers between devices, swapped(): return lax.ppermute(block, axis, route)  7.66 us
  transfers between devices with their start and end apart: 8, of which 7 were waited for; matrix products, arithmetic and copies ran while one was open for 1% of the time, Pallas kernels for 0%

commit v1 on v0

--- a/solution.py
+++ b/solution.py
@@ -1,7 +1,15 @@
+import functools
 import jax
 import jax.numpy as jnp
 from jax import lax
 from jax.sharding import PartitionSpec as P
+
+
+def deliver_sides(w_in, bus_axis):
+    return jax.lax.all_gather(w_in, bus_axis).sum(axis=0)
+
+
+_fill_shelves = functools.partial(deliver_sides, bus_axis="blk")
 
 
 def swapped(block, axis, apart):
@@ -15,7 +23,7 @@
 
 
 def group_sum(partial_value, height):
-    current = lax.psum(partial_value, "blk")
+    current = _fill_shelves(partial_value)
     for bit_number in range(height):
         current = current + swapped(current, "leaf", bit_number)
     return current

time: 353 us -> 254 us (0.72)
  waiting for transfers between devices: 143 us -> 8.9 us
  blocking collectives: 173 us -> 226 us
  between operations: 16.1 us -> 2.81 us
    all_gather x0 -> x5, blocking collectives: none -> 155 us  [deliver_sides(): return jax.lax.all_gather(w_in, bus_axis).sum(axis=0)]
    psum x2 -> x0, waiting for transfers between devices: 135 us -> none  [group_sum(): current = lax.psum(partial_value, 'blk')]
    psum x3 -> x0, blocking collectives: 102 us -> none  [group_sum(): current = lax.psum(partial_value, 'blk')]
  transfers between devices with their start and end apart: 8 -> 6, of which waited for: 7 -> 5; matrix products, arithmetic and copies ran while one was open for 1% -> 1% of each run, Pallas kernels for 0% -> 0%
where the time goes in v1:
time: 254 us
  blocking collectives  226 us (89%)
  matrix products  9.25 us (4%)
  waiting for transfers between devices  8.9 us (4%)
  local copies, waits for them, and re-layouts  3.11 us (1%)
  between operations  2.81 us (1%)
    all_gather x5, blocking collectives, deliver_sides(): return jax.lax.all_gather(w_in, bus_axis).sum(axis=0)  155 us
    all_gather x1, blocking collectives, local(): every_side = lax.all_gather(flat_side, ('leaf', 'blk'), axis=1, tiled=True)  71.1 us
    ppermute x6, waiting for transfers between devices, swapped(): return lax.ppermute(block, axis, route)  8.9 us
  transfers between devices with their start and end apart: 6, of which 5 were waited for; matrix products, arithmetic and copies ran while one was open for 1% of the time, Pallas kernels for 0%

profile of v1, /device:TPU:0, one launch (start us, length us, event | category | flops | bytes accessed | tf_op | source)
XLA Modules:
  0.0 253.9 jit_solution(12785789002883394261)
XLA Ops:
  0.6 71.1 %all-gather = f32[4,32,1,384]{3,2,1,0:T(1,128)S(1)} all-gather(f32[4,1,1,384]{3,2,1,0:T(1,128)} %param.4), channel_id=2, replica_groups=mesh['leaf'=4,'blk'=8] {'leaf','blk'}, dimensions={1}, use_global_device_ids=true | all-gather | bytes 202752 | tf_op jit(solution)/shard_map/all_gather | solution.py:43
  71.7 0.0 copy-start
  71.8 1.5 fusion.51
  73.3 0.6 compare_convert_fusion.2
  73.9 0.1 broadcast_bitcast_fusion.2
  74.7 1.1 convolution_multiply_fusion.1
  75.8 1.7 fusion.3
  77.5 30.7 %all-gather.6 = f32[8,4,2048]{2,1,0:T(4,128)S(1)} all-gather(f32[1,4,2048]{2,1,0:T(4,128)S(1)} %slice_bitcast_fusion.3), channel_id=3, replica_groups=mesh['leaf'=4,'blk'=8] {'blk'}, dimensions={0}, use_global_device_ids=true | all-gather | bytes 294912 | tf_op jit(solution)/shard_map/all_gather | solution.py:9
  108.3 0.1 collective-permute-start
  108.4 0.7 compare_convert_fusion.1
  109.1 0.1 broadcast_bitcast_fusion.1
  109.9 0.0 collective-permute-done
  109.9 0.0 copy-done
  109.9 0.2 convolution_multiply_fusion.2
  110.2 1.5 fusion
  111.7 31.3 %all-gather.7 = f32[8,4,4096]{2,1,0:T(4,128)S(1)} all-gather(f32[1,4,4096]{2,1,0:T(4,128)S(1)} %fusion), channel_id=4, replica_groups=mesh['leaf'=4,'blk'=8] {'blk'}, dimensions={0}, use_global_device_ids=true | all-gather | bytes 589824 | tf_op jit(solution)/shard_map/all_gather | solution.py:9
  142.9 0.1 reduce_sum.46
  143.0 0.1 collective-permute-start.1
  143.1 0.7 compare_convert_fusion
  143.8 0.6 collective-permute-done.1
  144.4 0.7 collective-permute-start.2
  145.1 0.1 broadcast_bitcast_fusion
  145.8 2.9 %collective-permute-done.2 = f32[4,4096]{1,0:T(4,128)S(1)} collective-permute-done((f32[4,4096]{1,0:T(4,128)S(1)}, f32[4,4096]{1,0:T(4,128)S(1)}, u32[]{:S(2)}, u32[]{:S(2)}) %collective-permute-start.2) | collective-permute-done | bytes 65568 | tf_op jit(solution)/shard_map/ppermute | solution.py:22
  148.7 0.4 convolution_multiply_fusion
  149.1 0.3 convolution_bitcast_fusion
  149.3 31.3 %all-gather.8 = f32[8,4,4096]{2,1,0:T(4,128)S(1)} all-gather(f32[1,4,4096]{2,1,0:T(4,128)S(1)} %convolution_bitcast_fusion), channel_id=5, replica_groups=mesh['leaf'=4,'blk'=8] {'blk'}, dimensions={0}, use_global_device_ids=true | all-gather | bytes 589824 | tf_op jit(solution)/shard_map/all_gather | solution.py:9
  180.7 0.1 reduce_sum.47
  180.7 0.1 collective-permute-start.3
  180.8 0.1 dynamic-slice
  180.9 1.2 collective-permute-done.3
  182.1 0.7 collective-permute-start.4
  182.8 0.6 copy.8
  183.4 3.0 %collective-permute-done.4 = f32[4,4096]{1,0:T(4,128)S(1)} collective-permute-done((f32[4,4096]{1,0:T(4,128)S(1)}, f32[4,4096]{1,0:T(4,128)S(1)}, u32[]{:S(2)}, u32[]{:S(2)}) %collective-permute-start.4) | collective-permute-done | bytes 65568 | tf_op jit(solution)/shard_map/ppermute | solution.py:22
  186.5 1.9 convolution_bitcast_fusion.1
  188.4 30.8 %all-gather.9 = f32[8,4,2048]{2,1,0:T(4,128)S(1)} all-gather(f32[1,4,2048]{2,1,0:T(4,128)S(1)} %convolution_bitcast_fusion.1), channel_id=6, replica_groups=mesh['leaf'=4,'blk'=8] {'blk'}, dimensions={0}, use_global_device_ids=true | all-gather | bytes 294912 | tf_op jit(solution)/shard_map/all_gather | solution.py:9
  219.2 0.1 collective-permute-start.5
  219.3 1.2 collective-permute-done.5
  220.5 2.1 convolution_bitcast_fusion.2
  222.6 30.6 %all-gather.10 = f32[8,4,1024]{2,1,0:T(4,128)S(1)} all-gather(f32[1,4,1024]{2,1,0:T(4,128)S(1)} %convolution_bitcast_fusion.2), channel_id=7, replica_groups=mesh['leaf'=4,'blk'=8] {'blk'}, dimensions={0}, use_global_device_ids=true | all-gather | bytes 147456 | tf_op jit(solution)/shard_map/all_gather | solution.py:9
  253.3 0.6 copy.9
  (17 shorter events, 0.4 us)
Async XLA Ops:
  71.7 38.2 %copy-start = (bf16[1,1,128,7168]{3,2,1,0:T(8,128)(2,1)S(1)}, bf16[1,1,128,7168]{3,2,1,0:T(8,128)(2,1)}, u32[]{:S(2)}) copy-start(bf16[1,1,128,7168]{3,2,1,0:T(8,128)(2,1)} %param.5) | copy-start | bytes 5505028
  108.3 1.6 collective-permute-start
  143.0 1.3 collective-permute-start.1
  144.4 4.3 %collective-permute-start.2 = (f32[4,4096]{1,0:T(4,128)S(1)}, f32[4,4096]{1,0:T(4,128)S(1)}, u32[]{:S(2)}, u32[]{:S(2)}) collective-permute-start(f32[4,4096]{1,0:T(4,128)S(1)} %add.65), channel_id=1, source_target_pairs={{0,16},{16,0},{8,24},{24,8},{1,17},{17,1},{9,25},{25,9},{2,18},{18... | collective-permute-start | bytes 196616 | tf_op jit(solution)/shard_map/ppermute | solution.py:22
  180.7 1.3 collective-permute-start.3
  182.1 4.3 %collective-permute-start.4 = (f32[4,4096]{1,0:T(4,128)S(1)}, f32[4,4096]{1,0:T(4,128)S(1)}, u32[]{:S(2)}, u32[]{:S(2)}) collective-permute-start(f32[4,4096]{1,0:T(4,128)S(1)} %add.67), channel_id=1, source_target_pairs={{0,16},{16,0},{8,24},{24,8},{1,17},{17,1},{9,25},{25,9},{2,18},{18... | collective-permute-start | bytes 196616 | tf_op jit(solution)/shard_map/ppermute | solution.py:22
  219.2 1.3 collective-permute-start.5
